TPU v7x, 32 devices: a whole 2x2x4 slice. The times are simulated.
32 devices in a mesh: ep: 8 (over z, x), dp: 4 (over y, core).
Axes of the slice: x: 2, y: 2, z: 4, core: 2. Of those that a mesh axis runs over, the one named last changes fastest.
Arguments:
- residual: bfloat16 [4096, 2880], P(('ep', 'dp')), may hold values from -400 to 400, as said below
- norm_gain: float32 [2880], replicated, may hold values from 0.25 to 1.75
- router_weight: bfloat16 [2880, 32], replicated, may hold values from -0.109375 to 0.109375
- out_grad: bfloat16 [4096, 2880], P(('ep', 'dp')), may hold values from -6 to 6
- expert_ids: int32 [4096, 4], P(('ep', 'dp')), may hold values from 0 to 31, all different within a row; in each aligned block of 128 rows (0 to 127, 128 to 255, ...) at most 24 rows name the same one
- hidden: bfloat16 [32, 768, 1440], P(('ep', 'dp')), may hold values from -0.3125 to 0.3125
- down_weight: bfloat16 [32, 1440, 2880], P(('ep', 'dp')), may hold values from -0.15625 to 0.15625
Outputs:
- hidden_grad: bfloat16 [32, 768, 1440], P(('ep', 'dp'))
- down_weight_grad: bfloat16 [32, 1440, 2880], P(('ep', 'dp'))
- residual_grad: bfloat16 [4096, 2880], P(('ep', 'dp'))
- router_grad: float32 [2880, 32], replicated
- gain_grad: float32 [2880], replicated
Inputs may be any that keep to these rules, and one draw needn't show every extreme that they name: `expert_ids`: in the tokens of one device no expert is named more than 24 times, a bound that some block reaches. `residual`: Real-valued entries.
All inputs are finite; a program needn't handle non-finite values.
Results may differ from a plain program's by a relative error of at most 0.0085.
Values may be sent and summed in bfloat16 or wider, within the bound.
A program may use at most 128 MiB of HBM per device.

v0:
```python
import jax
import jax.numpy as jnp
from jax import lax
from jax.sharding import PartitionSpec as P


def on_device(residual, norm_gain, router_weight, out_grad, expert_ids, hidden, down_weight):
    tokens_here, width = residual.shape
    top_count = expert_ids.shape[1]
    experts = router_weight.shape[1]
    slots = hidden.shape[1]
    capacity = slots // experts
    floated = residual.astype(jnp.float32)
    inverse = lax.rsqrt(jnp.mean(floated * floated, -1, keepdims=True) + 1e-05)
    unit = floated * inverse
    normed = (unit * norm_gain).astype(jnp.bfloat16)
    logits = jnp.dot(normed, router_weight, preferred_element_type=jnp.float32)
    match = expert_ids[:, :, None] == jnp.arange(experts, dtype=jnp.int32)[None, None, :]
    picked = jnp.sum(jnp.where(match, logits[:, None, :], jnp.float32(0.0)), -1)
    expo = jnp.exp(picked)
    prob = expo / jnp.sum(expo, -1, keepdims=True)
    flat_ids = expert_ids.reshape(-1)
    onehot = (flat_ids[:, None] == jnp.arange(experts, dtype=jnp.int32)[None, :]).astype(jnp.int32)
    slot_rank = jnp.sum((jnp.cumsum(onehot, 0) - onehot) * onehot, -1)
    place = flat_ids * capacity + slot_rank
    repeated = jnp.repeat(out_grad, top_count, axis=0)
    send_rows = jnp.zeros((experts * capacity, width), jnp.bfloat16).at[place].set(repeated)
    send_prob = (
        jnp.zeros((experts * capacity,), jnp.bfloat16)
        .at[place]
        .set(prob.astype(jnp.bfloat16).reshape(-1))
    )
    got_rows, got_prob = (
        lax.all_to_all(send_rows, ("ep", "dp"), split_axis=0, concat_axis=0, tiled=True),
        lax.all_to_all(send_prob, ("ep", "dp"), split_axis=0, concat_axis=0, tiled=True),
    )
    hidden_rows = hidden[0]
    weight = down_weight[0]
    inner = lax.dot_general(
        got_rows, weight, (((1,), (1,)), ((), ())), preferred_element_type=jnp.float32
    )
    slot_score = jnp.sum(inner * hidden_rows.astype(jnp.float32), -1)
    weight_col = got_prob.astype(jnp.float32)[:, None]
    hidden_grad = (weight_col * inner).astype(jnp.bfloat16)
    scaled = (weight_col * got_rows.astype(jnp.float32)).astype(jnp.bfloat16)
    weight_grad = lax.dot_general(
        hidden_rows, scaled, (((0,), (0,)), ((), ())), preferred_element_type=jnp.float32
    )
    came_back = lax.all_to_all(slot_score, ("ep", "dp"), split_axis=0, concat_axis=0, tiled=True)
    score = came_back[place].reshape(tokens_here, top_count)
    pick_grad = prob * (score - jnp.sum(prob * score, -1, keepdims=True))
    logit_grad = jnp.sum(jnp.where(match, pick_grad[:, :, None], jnp.float32(0.0)), 1)
    local_router = jnp.dot(
        normed.astype(jnp.float32).T, logit_grad, precision=lax.Precision.HIGHEST
    )
    normed_grad = jnp.dot(
        logit_grad, router_weight.astype(jnp.float32).T, precision=lax.Precision.HIGHEST
    )
    local_gain = jnp.sum(normed_grad * unit, 0)
    router_grad, gain_grad = lax.psum((local_router, local_gain), ("ep", "dp"))
    upper = normed_grad * norm_gain
    residual_grad = (inverse * (upper - unit * jnp.mean(upper * unit, -1, keepdims=True))).astype(
        jnp.bfloat16
    )
    return (
        hidden_grad[None],
        weight_grad.astype(jnp.bfloat16)[None],
        residual_grad,
        router_grad,
        gain_grad,
    )


def solution(mesh):
    return jax.shard_map(
        on_device,
        mesh=mesh,
        in_specs=(
            P(("ep", "dp"), None),
            P(),
            P(),
            P(("ep", "dp"), None),
            P(("ep", "dp"), None),
            P(("ep", "dp"), None, None),
            P(("ep", "dp"), None, None),
        ),
        out_specs=(
            P(("ep", "dp"), None, None),
            P(("ep", "dp"), None, None),
            P(("ep", "dp"), None),
            P(),
            P(),
        ),
        check_vma=False,
    )
```

profile of v0, /device:TPU:0, one launch (start us, length us, event | category | flops | bytes accessed | tf_op | source)
XLA Modules:
  0.0 325.0 jit_solution(3421626252912884726)
XLA Ops:
  7.2 0.0 copy-start
  7.2 0.0 copy-start.3
  7.2 0.8 broadcast_multiply_fusion
  8.0 0.8 copy.37
  8.8 0.1 eq.38
  8.9 0.1 eq.42
  9.0 0.1 copy.36
  9.1 0.1 mul.96
  9.2 1.2 reduce-window.6
  10.4 0.2 slice_reduce_fusion
  10.6 1.5 fusion.17
  12.2 1.7 fusion.20
  13.9 0.1 copy.40
  14.1 0.1 reshape.161
  14.2 0.1 fusion.24
  14.3 3.8 %scatter_custom_fusion = bf16[768]{0:T(1024)(128)(2,1)S(1)} fusion(s32[512]{0:T(512)S(1)} %bitcast.53, bf16[512]{0:T(512)(128)(2,1)S(1)} %reshape.161, bf16[]{:T(256)} %constant.7.clone.1), kind=kCustom, calls=%fused_computation.49 | custom fusion | bytes 1538 | tf_op jit(solution)/shard_map/scatter | solution.py:31
  18.1 0.7 all_to_all.30
  18.8 7.3 %all-to-all-start = ((bf16[32,24,1]{1,2,0:T(2,128)(2,1)}), bf16[32,24,1]{1,2,0:T(2,128)(2,1)S(1)}, u32[]{:S(2)}, u32[]{:S(2)}) async-start(bf16[32,24,1]{1,2,0:T(2,128)(2,1)} %all_to_all.30), calls=%async_computation | async-start | bytes 32768 | tf_op jit(solution)/shard_map/all_to_all | solution.py:35
  26.1 1.2 copy.44
  27.3 1.9 broadcast_in_dim.56
  29.2 2.9 reshape.169
  32.1 8.8 %scatter_custom_fusion.1 = bf16[768,2880]{1,0:T(8,128)(2,1)} fusion(s32[512]{0:T(512)S(1)} %bitcast.54, bf16[512,2880]{1,0:T(8,128)(2,1)} %reshape.169, bf16[]{:T(256)} %constant.7.clone.1), kind=kCustom, calls=%fused_computation.10 | custom fusion | bytes 4424192 | tf_op jit(solution)/shard_map/scatter | solution.py:27
  40.9 5.9 %all-to-all-start.1 = ((bf16[32,24,2880]{2,1,0:T(8,128)(2,1)}), bf16[32,24,2880]{2,1,0:T(8,128)(2,1)}, u32[]{:S(2)}, u32[]{:S(2)}) async-start(bf16[32,24,2880]{2,1,0:T(8,128)(2,1)} %bitcast.51), calls=%async_computation.1 | async-start | bytes 9043968 | tf_op jit(solution)/shard_map/all_to_all | solution.py:34
  46.8 0.1 copy.42
  46.9 0.1 copy.43
  47.0 0.1 reshape.147
  47.1 0.1 copy.45
  47.2 100.9 %all-to-all-done.1 = bf16[32,24,2880]{2,1,0:T(8,128)(2,1)} async-done(((bf16[32,24,2880]{2,1,0:T(8,128)(2,1)}), bf16[32,24,2880]{2,1,0:T(8,128)(2,1)}, u32[]{:S(2)}, u32[]{:S(2)}) %all-to-all-start.1) | async-done | bytes 4423712 | tf_op jit(solution)/shard_map/all_to_all | solution.py:34
  148.1 12.2 %multiply_reduce_fusion = (f32[768]{0:T(1024)S(1)}, bf16[1,768,1440]{1,2,0:T(8,128)(2,1)}) fusion(bf16[1,768,1440]{1,2,0:T(8,128)(2,1)} %param.12, f32[768]{0:T(1024)S(1)} %reshape.147, bf16[768,2880]{1,0:T(8,128)(2,1)} %bitcast.4, bf16[1,1440,2880]{2,1,0:T(8,128)(2,1)} %param.13), kind=kOutput, calls=%fused_computation.8 | convolution fusion | flops 6375627776 | bytes 17147904 | tf_op jit(solution)/shard_map/dot_general | solution.py:39
  160.3 0.7 all_to_all.27
  161.0 5.2 %all-to-all-start.2 = ((f32[32,24,1]{1,2,0:T(1,128)}), f32[32,24,1]{1,2,0:T(1,128)S(1)}, u32[]{:S(2)}, u32[]{:S(2)}) async-start(f32[32,24,1]{1,2,0:T(1,128)} %bitcast.12), calls=%async_computation.2 | async-start | bytes 32768 | tf_op jit(solution)/shard_map/all_to_all | solution.py:49
  166.2 0.0 all-reduce.2.cloned.1.call-start
  166.3 0.0 copy-start.5
  166.3 3.8 %multiply_convert_fusion = bf16[32,24,2880]{2,1,0:T(8,128)(2,1)S(1)} fusion(bf16[32,24,2880]{2,1,0:T(8,128)(2,1)} %all-to-all-done.1, f32[32,24]{1,0:T(8,128)S(1)} %copy.45), kind=kLoop, calls=%fused_computation.5 | loop fusion | flops 6635520 | bytes 8850432 | tf_op jit(solution)/shard_map/convert_element_type | solution.py:45
  170.1 9.3 %fusion = bf16[1,1440,2880]{2,1,0:T(8,128)(2,1)} fusion(bf16[768,2880]{1,0:T(8,128)(2,1)S(1)} %bitcast.52, bf16[1,768,1440]{1,2,0:T(8,128)(2,1)S(1)} %copy-done.5), kind=kOutput, calls=%fused_computation.4 | convolution fusion | flops 6374246400 | bytes 14929920 | tf_op jit(solution)/shard_map/dot_general | solution.py:46
  179.4 0.5 broadcast.113
  179.9 0.7 reduce.5
  180.6 0.1 all_to_all.29
  180.7 2.3 gather_fusion
  183.0 0.1 reshape.146
  183.1 0.1 copy.48
  183.3 1.7 fusion.16
  184.9 1.8 fusion.18
  186.7 0.0 all-reduce.2.cloned.1.call-update
  186.8 1.3 fusion.15
  188.1 40.6 %psum.15 = f32[2880]{0:T(1024)} all-reduce(f32[2880]{0:T(1024)S(1)} %get-tuple-element.5), channel_id=1, replica_groups=mesh['ep'=8,'dp'=4] {'ep','dp'}, use_global_device_ids=true, to_apply=%region_14.15 | all-reduce | flops 2880 | bytes 23040 | tf_op jit(solution)/shard_map/psum | solution.py:60
  228.7 87.7 %all-reduce.2.cloned.1.call-done = f32[2880,32]{0,1:T(8,128)} async-done(((f32[2880,32]{0,1:T(8,128)}), f32[2880,32]{0,1:T(8,128)}) %all-reduce.2.cloned.1.call-update) | async-done | bytes 368656 | tf_op jit(solution)/shard_map/psum | solution.py:60
  316.4 1.8 copy.52
  (25 shorter events, 0.2 us)
Async XLA Ops:
  7.2 5.0 %copy-start = (bf16[2880,32]{0,1:T(8,128)(2,1)S(1)}, bf16[2880,32]{0,1:T(8,128)(2,1)}, u32[]{:S(2)}) copy-start(bf16[2880,32]{0,1:T(8,128)(2,1)} %param.9) | copy-start | bytes 552964
  7.2 6.7 %copy-start.3 = (s32[128,4]{0,1:T(4,128)S(1)}, s32[128,4]{0,1:T(4,128)}, u32[]{:S(2)}) copy-start(s32[128,4]{0,1:T(4,128)} %param.11) | copy-start | bytes 6148
  7.2 18.9 %copy-start.2 = (bf16[128,2880]{0,1:T(8,128)(2,1)S(1)}, bf16[128,2880]{0,1:T(8,128)(2,1)}, u32[]{:S(2)}) copy-start(bf16[128,2880]{0,1:T(8,128)(2,1)} %param.10) | copy-start | bytes 2211844
  18.8 22.1 %all-to-all-start = ((bf16[32,24,1]{1,2,0:T(2,128)(2,1)}), bf16[32,24,1]{1,2,0:T(2,128)(2,1)S(1)}, u32[]{:S(2)}, u32[]{:S(2)}) async-start(bf16[32,24,1]{1,2,0:T(2,128)(2,1)} %all_to_all.30), calls=%async_computation | async-start | bytes 32768 | tf_op jit(solution)/shard_map/all_to_all | solution.py:35
  40.9 107.3 %all-to-all-start.1 = ((bf16[32,24,2880]{2,1,0:T(8,128)(2,1)}), bf16[32,24,2880]{2,1,0:T(8,128)(2,1)}, u32[]{:S(2)}, u32[]{:S(2)}) async-start(bf16[32,24,2880]{2,1,0:T(8,128)(2,1)} %bitcast.51), calls=%async_computation.1 | async-start | bytes 9043968 | tf_op jit(solution)/shard_map/all_to_all | solution.py:34
  161.0 18.4 %all-to-all-start.2 = ((f32[32,24,1]{1,2,0:T(1,128)}), f32[32,24,1]{1,2,0:T(1,128)S(1)}, u32[]{:S(2)}, u32[]{:S(2)}) async-start(f32[32,24,1]{1,2,0:T(1,128)} %bitcast.12), calls=%async_computation.2 | async-start | bytes 32768 | tf_op jit(solution)/shard_map/all_to_all | solution.py:49
  166.2 150.2 %all-reduce.2.cloned.1.call-start = ((), (), s32[]{:S(2)}) async-start(), calls=%async_computation.3 | async-start | bytes 753664 | tf_op jit(solution)/shard_map/psum | solution.py:60
  166.3 3.9 %copy-start.5 = (bf16[1,768,1440]{1,2,0:T(8,128)(2,1)S(1)}, bf16[1,768,1440]{1,2,0:T(8,128)(2,1)}, u32[]{:S(2)}) copy-start(bf16[1,768,1440]{1,2,0:T(8,128)(2,1)} %param.12) | copy-start | bytes 6635524
  179.4 3.8 %copy-start.1 = (bf16[128,2880]{0,1:T(8,128)(2,1)S(1)}, bf16[128,2880]{0,1:T(8,128)(2,1)}, u32[]{:S(2)}) copy-start(bf16[128,2880]{0,1:T(8,128)(2,1)} %param.7) | copy-start | bytes 2211844
  179.4 3.9 %copy-start.4 = (f32[2880]{0:T(1024)S(1)}, f32[2880]{0:T(1024)}, u32[]{:S(2)}) copy-start(f32[2880]{0:T(1024)} %param.8) | copy-start | bytes 34564
Sparse Core Ops, SparseCore 0:
  186.9 129.4 all-reduce.1
where the time goes:
time: 326 us; the launch traced here: 325 us
  waiting for transfers between devices  189 us (58%)
  blocking collectives  40.6 us (12%)
  local copies, waits for them, and re-layouts  26.7 us (8%)
  matrix products  26.6 us (8%)
  starting transfers between devices  18.5 us (6%)
  between operations  14.3 us (4%)
  other arithmetic  9.59 us (3%)
    all_to_all x1, waiting for transfers between devices, on_device(): lax.all_to_all(send_rows, ('ep', 'dp'), split_axis=0, concat_axis=0, tile...  101 us
    psum x1, waiting for transfers between devices, on_device(): router_grad, gain_grad = lax.psum((local_router, local_gain), ('ep', 'dp'))  87.7 us
    psum x1, blocking collectives, on_device(): router_grad, gain_grad = lax.psum((local_router, local_gain), ('ep', 'dp'))  40.6 us
    dot_general x1, matrix products, on_device(): lax.dot_general(got_rows, weight, (((1,), (1,)), ((), ())), preferred_ele...  12.2 us
    dot_general x1, matrix products, on_device(): lax.dot_general(hidden_rows, scaled, (((0,), (0,)), ((), ())), preferred_...  9.29 us
    scatter x1, local copies, waits for them, and re-layouts, on_device(): jnp.zeros((experts * capacity, width), jnp.bfloat16).at[place].set(repeated)  8.78 us
    all_to_all x1, starting transfers between devices, on_device(): lax.all_to_all(send_prob, ('ep', 'dp'), split_axis=0, concat_axis=0, tile...  7.33 us
  transfers between devices with their start and end apart: 4, of which 2 were waited for; matrix products, arithmetic and copies ran while one was open for 9% of the time, Pallas kernels for 0%

commit v1 on v0

--- a/solution.py
+++ b/solution.py
@@ -57,7 +57,7 @@
         logit_grad, router_weight.astype(jnp.float32).T, precision=lax.Precision.HIGHEST
     )
     local_gain = jnp.sum(normed_grad * unit, 0)
-    router_grad, gain_grad = lax.psum((local_router, local_gain), ("ep", "dp"))
+    router_grad, gain_grad = lax.psum(lax.psum((local_router, local_gain), "dp"), "ep")
     upper = normed_grad * norm_gain
     residual_grad = (inverse * (upper - unit * jnp.mean(upper * unit, -1, keepdims=True))).astype(
         jnp.bfloat16

time: 326 us -> 305 us (0.936)
  waiting for transfers between devices: 189 us -> 161 us
  blocking collectives: 40.6 us -> 47.6 us
    psum x1 -> x2, waiting for transfers between devices: 87.7 us -> 60.1 us  [the longest x1 33.8 us: on_device(): lax.psum((local_router, local_gain), 'dp')]
    psum x1 -> x2, blocking collectives: 40.6 us -> 47.6 us  [the longest x1 37.5 us: on_device(): lax.psum(lax.psum((local_router, local_gain), 'dp'), 'ep')]
  transfers between devices with their start and end apart: 4 -> 5, of which waited for: 2 -> 3; matrix products, arithmetic and copies ran while one was open for 9% -> 10% of each run, Pallas kernels for 0% -> 0%
where the time goes in v1:
time: 305 us; the launch traced here: 304 us
  waiting for transfers between devices  161 us (53%)
  blocking collectives  47.6 us (16%)
  local copies, waits for them, and re-layouts  26.7 us (9%)
  matrix products  26.6 us (9%)
  starting transfers between devices  18.5 us (6%)
  between operations  14.3 us (5%)
  other arithmetic  9.59 us (3%)
    all_to_all x1, waiting for transfers between devices, on_device(): lax.all_to_all(send_rows, ('ep', 'dp'), split_axis=0, concat_axis=0, tile...  101 us
    psum x1, blocking collectives, on_device(): lax.psum(lax.psum((local_router, local_gain), 'dp'), 'ep')  37.5 us
    psum x1, waiting for transfers between devices, on_device(): lax.psum((local_router, local_gain), 'dp')  33.8 us
    psum x1, waiting for transfers between devices, on_device(): lax.psum(lax.psum((local_router, local_gain), 'dp'), 'ep')  26.3 us
    dot_general x1, matrix products, on_device(): lax.dot_general(got_rows, weight, (((1,), (1,)), ((), ())), preferred_ele...  12.2 us
    psum x1, blocking collectives, on_device(): lax.psum((local_router, local_gain), 'dp')  10.1 us
    dot_general x1, matrix products, on_device(): lax.dot_general(hidden_rows, scaled, (((0,), (0,)), ((), ())), preferred_...  9.29 us
    scatter x1, local copies, waits for them, and re-layouts, on_device(): jnp.zeros((experts * capacity, width), jnp.bfloat16).at[place].set(repeated)  8.78 us
  transfers between devices with their start and end apart: 5, of which 3 were waited for; matrix products, arithmetic and copies ran while one was open for 10% of the time, Pallas kernels for 0%

profile of v1, /device:TPU:0, one launch (start us, length us, event | category | flops | bytes accessed | tf_op | source)
XLA Modules:
  0.0 304.5 jit_solution(6148173621931066230)
XLA Ops:
  7.2 0.8 broadcast_multiply_fusion
  8.0 0.8 copy.37
  8.8 0.1 eq.38
  8.9 0.1 eq.42
  9.0 0.1 copy.36
  9.1 0.1 mul.96
  9.2 1.2 reduce-window.6
  10.4 0.2 slice_reduce_fusion
  10.6 1.5 fusion.17
  12.2 1.7 fusion.20
  13.9 0.1 copy.40
  14.1 0.1 reshape.161
  14.2 0.1 fusion.24
  14.3 3.8 %scatter_custom_fusion = bf16[768]{0:T(1024)(128)(2,1)S(1)} fusion(s32[512]{0:T(512)S(1)} %bitcast.53, bf16[512]{0:T(512)(128)(2,1)S(1)} %reshape.161, bf16[]{:T(256)} %constant.7.clone.1), kind=kCustom, calls=%fused_computation.49 | custom fusion | bytes 1538 | tf_op jit(solution)/shard_map/scatter | solution.py:31
  18.1 0.7 all_to_all.30
  18.8 7.3 %all-to-all-start = ((bf16[32,24,1]{1,2,0:T(2,128)(2,1)}), bf16[32,24,1]{1,2,0:T(2,128)(2,1)S(1)}, u32[]{:S(2)}, u32[]{:S(2)}) async-start(bf16[32,24,1]{1,2,0:T(2,128)(2,1)} %all_to_all.30), calls=%async_computation | async-start | bytes 32768 | tf_op jit(solution)/shard_map/all_to_all | solution.py:35
  26.1 1.2 copy.44
  27.3 1.9 broadcast_in_dim.56
  29.2 2.9 reshape.169
  32.1 8.8 %scatter_custom_fusion.1 = bf16[768,2880]{1,0:T(8,128)(2,1)} fusion(s32[512]{0:T(512)S(1)} %bitcast.54, bf16[512,2880]{1,0:T(8,128)(2,1)} %reshape.169, bf16[]{:T(256)} %constant.7.clone.1), kind=kCustom, calls=%fused_computation.10 | custom fusion | bytes 4424192 | tf_op jit(solution)/shard_map/scatter | solution.py:27
  40.9 5.9 %all-to-all-start.1 = ((bf16[32,24,2880]{2,1,0:T(8,128)(2,1)}), bf16[32,24,2880]{2,1,0:T(8,128)(2,1)}, u32[]{:S(2)}, u32[]{:S(2)}) async-start(bf16[32,24,2880]{2,1,0:T(8,128)(2,1)} %bitcast.51), calls=%async_computation.1 | async-start | bytes 9043968 | tf_op jit(solution)/shard_map/all_to_all | solution.py:34
  46.8 0.1 copy.42
  46.9 0.1 copy.43
  47.0 0.1 reshape.147
  47.1 0.1 copy.45
  47.2 100.9 %all-to-all-done.1 = bf16[32,24,2880]{2,1,0:T(8,128)(2,1)} async-done(((bf16[32,24,2880]{2,1,0:T(8,128)(2,1)}), bf16[32,24,2880]{2,1,0:T(8,128)(2,1)}, u32[]{:S(2)}, u32[]{:S(2)}) %all-to-all-start.1) | async-done | bytes 4423712 | tf_op jit(solution)/shard_map/all_to_all | solution.py:34
  148.1 12.2 %multiply_reduce_fusion = (f32[768]{0:T(1024)S(1)}, bf16[1,768,1440]{1,2,0:T(8,128)(2,1)}) fusion(bf16[1,768,1440]{1,2,0:T(8,128)(2,1)} %param.12, f32[768]{0:T(1024)S(1)} %reshape.147, bf16[768,2880]{1,0:T(8,128)(2,1)} %bitcast.4, bf16[1,1440,2880]{2,1,0:T(8,128)(2,1)} %param.13), kind=kOutput, calls=%fused_computation.8 | convolution fusion | flops 6375627776 | bytes 17147904 | tf_op jit(solution)/shard_map/dot_general | solution.py:39
  160.3 0.7 all_to_all.27
  161.0 5.2 %all-to-all-start.2 = ((f32[32,24,1]{1,2,0:T(1,128)}), f32[32,24,1]{1,2,0:T(1,128)S(1)}, u32[]{:S(2)}, u32[]{:S(2)}) async-start(f32[32,24,1]{1,2,0:T(1,128)} %bitcast.12), calls=%async_computation.2 | async-start | bytes 32768 | tf_op jit(solution)/shard_map/all_to_all | solution.py:49
  166.2 0.0 all-reduce.3.cloned.1.call-start
  166.3 3.8 %multiply_convert_fusion = bf16[32,24,2880]{2,1,0:T(8,128)(2,1)S(1)} fusion(bf16[32,24,2880]{2,1,0:T(8,128)(2,1)} %all-to-all-done.1, f32[32,24]{1,0:T(8,128)S(1)} %copy.45), kind=kLoop, calls=%fused_computation.5 | loop fusion | flops 6635520 | bytes 8850432 | tf_op jit(solution)/shard_map/convert_element_type | solution.py:45
  170.1 9.3 %fusion = bf16[1,1440,2880]{2,1,0:T(8,128)(2,1)} fusion(bf16[768,2880]{1,0:T(8,128)(2,1)S(1)} %bitcast.52, bf16[1,768,1440]{1,2,0:T(8,128)(2,1)S(1)} %copy-done.5), kind=kOutput, calls=%fused_computation.4 | convolution fusion | flops 6374246400 | bytes 14929920 | tf_op jit(solution)/shard_map/dot_general | solution.py:46
  179.4 0.5 broadcast.113
  179.9 0.7 reduce.5
  180.6 0.1 all_to_all.29
  180.7 2.3 gather_fusion
  183.0 0.1 reshape.146
  183.1 0.1 copy.48
  183.3 1.7 fusion.16
  184.9 1.8 fusion.18
  186.8 0.0 all-reduce.5.cloned.1.call-start
  186.8 33.8 %all-reduce.3.cloned.1.call-done = f32[2880,32]{0,1:T(8,128)} async-done(((f32[2880,32]{0,1:T(8,128)}), f32[2880,32]{0,1:T(8,128)}) %all-reduce.3.cloned.1.call-update) | async-done | bytes 368656 | tf_op jit(solution)/shard_map/psum | solution.py:60
  220.7 0.0 all-reduce.5.cloned.1.call-update
  220.7 1.3 fusion.15
  222.0 10.1 %psum.30 = f32[2880]{0:T(1024)S(1)} all-reduce(f32[2880]{0:T(1024)S(1)} %get-tuple-element.5), channel_id=1, replica_groups=mesh['ep'=8,'dp'=4] {'dp'}, use_global_device_ids=true, to_apply=%region_15.16 | all-reduce | flops 2880 | bytes 23040 | tf_op jit(solution)/shard_map/psum | solution.py:60
  232.1 37.5 %psum.31 = f32[2880]{0:T(1024)} all-reduce(f32[2880]{0:T(1024)S(1)} %psum.30), channel_id=1, replica_groups=mesh['ep'=8,'dp'=4] {'ep'}, use_global_device_ids=true, to_apply=%region_16.17 | all-reduce | flops 2880 | bytes 23040 | tf_op jit(solution)/shard_map/psum | solution.py:60
  269.6 26.3 %all-reduce.5.cloned.1.call-done = f32[2880,32]{0,1:T(8,128)} async-done(((f32[2880,32]{0,1:T(8,128)}), f32[2880,32]{0,1:T(8,128)}) %all-reduce.5.cloned.1.call-update) | async-done | bytes 368656 | tf_op jit(solution)/shard_map/psum | solution.py:60
  295.9 1.8 copy.53
  (29 shorter events, 0.3 us)
Async XLA Ops:
  7.2 5.0 %copy-start = (bf16[2880,32]{0,1:T(8,128)(2,1)S(1)}, bf16[2880,32]{0,1:T(8,128)(2,1)}, u32[]{:S(2)}) copy-start(bf16[2880,32]{0,1:T(8,128)(2,1)} %param.9) | copy-start | bytes 552964
  7.2 6.7 %copy-start.3 = (s32[128,4]{0,1:T(4,128)S(1)}, s32[128,4]{0,1:T(4,128)}, u32[]{:S(2)}) copy-start(s32[128,4]{0,1:T(4,128)} %param.11) | copy-start | bytes 6148
  7.2 18.9 %copy-start.2 = (bf16[128,2880]{0,1:T(8,128)(2,1)S(1)}, bf16[128,2880]{0,1:T(8,128)(2,1)}, u32[]{:S(2)}) copy-start(bf16[128,2880]{0,1:T(8,128)(2,1)} %param.10) | copy-start | bytes 2211844
  18.8 22.1 %all-to-all-start = ((bf16[32,24,1]{1,2,0:T(2,128)(2,1)}), bf16[32,24,1]{1,2,0:T(2,128)(2,1)S(1)}, u32[]{:S(2)}, u32[]{:S(2)}) async-start(bf16[32,24,1]{1,2,0:T(2,128)(2,1)} %all_to_all.30), calls=%async_computation | async-start | bytes 32768 | tf_op jit(solution)/shard_map/all_to_all | solution.py:35
  40.9 107.3 %all-to-all-start.1 = ((bf16[32,24,2880]{2,1,0:T(8,128)(2,1)}), bf16[32,24,2880]{2,1,0:T(8,128)(2,1)}, u32[]{:S(2)}, u32[]{:S(2)}) async-start(bf16[32,24,2880]{2,1,0:T(8,128)(2,1)} %bitcast.51), calls=%async_computation.1 | async-start | bytes 9043968 | tf_op jit(solution)/shard_map/all_to_all | solution.py:34
  161.0 18.4 %all-to-all-start.2 = ((f32[32,24,1]{1,2,0:T(1,128)}), f32[32,24,1]{1,2,0:T(1,128)S(1)}, u32[]{:S(2)}, u32[]{:S(2)}) async-start(f32[32,24,1]{1,2,0:T(1,128)} %bitcast.12), calls=%async_computation.2 | async-start | bytes 32768 | tf_op jit(solution)/shard_map/all_to_all | solution.py:49
  166.2 54.4 %all-reduce.3.cloned.1.call-start = ((), (), s32[]{:S(2)}) async-start(), calls=%async_computation.3 | async-start | bytes 753664 | tf_op jit(solution)/shard_map/psum | solution.py:60
  166.3 3.9 %copy-start.5 = (bf16[1,768,1440]{1,2,0:T(8,128)(2,1)S(1)}, bf16[1,768,1440]{1,2,0:T(8,128)(2,1)}, u32[]{:S(2)}) copy-start(bf16[1,768,1440]{1,2,0:T(8,128)(2,1)} %param.12) | copy-start | bytes 6635524
  179.4 3.8 %copy-start.1 = (bf16[128,2880]{0,1:T(8,128)(2,1)S(1)}, bf16[128,2880]{0,1:T(8,128)(2,1)}, u32[]{:S(2)}) copy-start(bf16[128,2880]{0,1:T(8,128)(2,1)} %param.7) | copy-start | bytes 2211844
  179.4 3.9 %copy-start.4 = (f32[2880]{0:T(1024)S(1)}, f32[2880]{0:T(1024)}, u32[]{:S(2)}) copy-start(f32[2880]{0:T(1024)} %param.8) | copy-start | bytes 34564
  186.8 109.1 %all-reduce.5.cloned.1.call-start = ((), (), s32[]{:S(2)}) async-start(), calls=%async_computation.4 | async-start | bytes 753664 | tf_op jit(solution)/shard_map/psum | solution.py:60
Sparse Core Ops, SparseCore 0:
  186.9 33.7 all-reduce.2
  224.0 71.8 all-reduce.4
